TPU v7x, 8 devices: a whole 2x2x1 slice. The times are simulated.
8 devices in a mesh: replica: 1 (over z), ep: 8 (over y, x, core).
Axes of the slice: x: 2, y: 2, z: 1, core: 2. Of those that a mesh axis runs over, the one named last changes fastest.
Arguments:
- tok_in: bfloat16 [4096, 2048], P(('replica', 'ep'))
- routes: int32 [2, 4096, 8], P(None, ('replica', 'ep'))
- gate_vals: float32 [2, 4096, 8], P(None, ('replica', 'ep'))
- w_gate: bfloat16 [2, 16, 2048, 1024], P(None, ('replica', 'ep'))
- w_up: bfloat16 [2, 16, 2048, 1024], P(None, ('replica', 'ep'))
- w_down: bfloat16 [2, 16, 1024, 2048], P(None, ('replica', 'ep'))
- sh_gate: bfloat16 [2, 2048, 1024], replicated
- sh_up: bfloat16 [2, 2048, 1024], replicated
- sh_down: bfloat16 [2, 1024, 2048], replicated
- old_map: int32 [2, 16], P(None, 'replica')
- move_slot: int32 [2, 2], P(None, 'replica')
- move_expert: int32 [2, 2], P(None, 'replica')
Outputs:
- output 1: bfloat16 [4096, 2048], P(('replica', 'ep'))
- output 2: bfloat16 [2, 16, 2048, 1024], P(None, ('replica', 'ep'))
- output 3: bfloat16 [2, 16, 2048, 1024], P(None, ('replica', 'ep'))
- output 4: bfloat16 [2, 16, 1024, 2048], P(None, ('replica', 'ep'))
All inputs are finite; a program needn't handle non-finite values.
Results may differ from a plain program's by a relative error of at most 0.0116165.
Values are sent between devices in bfloat16 or wider.
A program may use at most 1 GiB of HBM per device.

v0:
```python
import jax
import jax.numpy as jnp
from jax import lax
from jax.sharding import PartitionSpec as P

TOKEN_AXES = ('replica', 'ep')


def first_holder(slot_map, wanted):
    slot_ids = jnp.arange(slot_map.shape[0], dtype=jnp.int32)
    hit_mask = slot_map[None, :] == wanted[:, None]
    return jnp.min(jnp.where(hit_mask, slot_ids[None, :], slot_map.shape[0]), axis=1)


def swiglu(hidden, w_gate, w_up, w_down):
    gate_proj = jnp.dot(hidden, w_gate, preferred_element_type=jnp.float32)
    up_proj = jnp.dot(hidden, w_up, preferred_element_type=jnp.float32)
    inner_act = (jax.nn.silu(gate_proj) * up_proj).astype(jnp.bfloat16)
    return jnp.dot(inner_act, w_down, preferred_element_type=jnp.float32)


def send_moved(weights, slot_map, move_expert, slots_dev, my_dev):
    source = first_holder(slot_map, move_expert)
    is_source = (source // slots_dev) == my_dev
    local_idx = source % slots_dev
    return tuple(jnp.where(is_source[:, None, None], jnp.take(weight_arr, local_idx, axis=0), jnp.zeros((), weight_arr.dtype)) for weight_arr in weights)


def place_moved(weights, arrived, move_slot, slots_dev, my_dev):
    local_ids = my_dev * slots_dev + jnp.arange(slots_dev, dtype=jnp.int32)
    match_mask = (move_slot[None, :] == local_ids[:, None]).astype(jnp.int32)
    is_target = jnp.max(match_mask, axis=1) > 0
    pick_idx = jnp.argmax(match_mask, axis=1)
    return tuple(jnp.where(is_target[:, None, None], jnp.take(arrived_arr, pick_idx, axis=0), weight_arr) for arrived_arr, weight_arr in zip(arrived, weights))


def moe_layer(hidden, route_all, gate_all, expert_w, shared_w, slot_map, slots_dev, my_dev):
    gathered = lax.all_gather(hidden, 'ep', axis=0, tiled=True)
    slot_ids = jnp.arange(slot_map.shape[0], dtype=jnp.int32)
    serve_all = (first_holder(slot_map, slot_map) == slot_ids).astype(jnp.float32)
    local_map = lax.dynamic_slice_in_dim(slot_map, my_dev * slots_dev, slots_dev)
    local_serve = lax.dynamic_slice_in_dim(serve_all, my_dev * slots_dev, slots_dev)
    hit_mask = route_all[:, :, None] == local_map[None, None, :]
    gate_coef = jnp.sum(jnp.where(hit_mask, gate_all[:, :, None], 0.0), axis=1) * local_serve[None, :]
    gate_proj = jnp.einsum('nd,jdf->jnf', gathered, expert_w[0], preferred_element_type=jnp.float32)
    up_proj = jnp.einsum('nd,jdf->jnf', gathered, expert_w[1], preferred_element_type=jnp.float32)
    inner_act = (jax.nn.silu(gate_proj) * up_proj).astype(jnp.bfloat16)
    expert_out = jnp.einsum('jnf,jfd->jnd', inner_act, expert_w[2], preferred_element_type=jnp.float32)
    partial_sum = jnp.sum(expert_out * gate_coef.T[:, :, None], axis=0)
    combined = lax.psum_scatter(partial_sum, 'ep', scatter_dimension=0, tiled=True)
    shared_out = swiglu(hidden, shared_w[0], shared_w[1], shared_w[2])
    return (hidden.astype(jnp.float32) + shared_out + combined).astype(jnp.bfloat16)


def solution(mesh):
    def body(tok_in, routes, gate_vals, w_gate, w_up, w_down, sh_gate, sh_up, sh_down, old_map, move_slot, move_expert):
        my_dev = lax.axis_index('ep')
        slots_dev = w_gate.shape[1]
        route_all = lax.all_gather(routes, 'ep', axis=1, tiled=True)
        gate_all = lax.all_gather(gate_vals, 'ep', axis=1, tiled=True)
        hidden = tok_in
        placed = []
        for layer_idx in range(2):
            layer_w = (w_gate[layer_idx], w_up[layer_idx], w_down[layer_idx])
            outgoing = send_moved(layer_w, old_map[layer_idx], move_expert[layer_idx], slots_dev, my_dev)
            arrived = lax.psum(outgoing, 'ep')
            new_w = place_moved(layer_w, arrived, move_slot[layer_idx], slots_dev, my_dev)
            new_map = old_map[layer_idx].at[move_slot[layer_idx]].set(move_expert[layer_idx])
            shared_w = (sh_gate[layer_idx], sh_up[layer_idx], sh_down[layer_idx])
            hidden = moe_layer(hidden, route_all[layer_idx], gate_all[layer_idx], new_w, shared_w, new_map, slots_dev, my_dev)
            placed.append(new_w)
        new_gate = jnp.stack([placed[0][0], placed[1][0]])
        new_up = jnp.stack([placed[0][1], placed[1][1]])
        new_down = jnp.stack([placed[0][2], placed[1][2]])
        return (hidden, new_gate, new_up, new_down)

    weight_spec = P(None, TOKEN_AXES, None, None)
    route_spec = P(None, TOKEN_AXES, None)
    map_spec = P(None, 'replica')
    shared_spec = P(None, None, None)
    tok_spec = P(TOKEN_AXES, None)
    return jax.shard_map(body, mesh=mesh, in_specs=(tok_spec, route_spec, route_spec, weight_spec, weight_spec, weight_spec, shared_spec, shared_spec, shared_spec, map_spec, map_spec, map_spec), out_specs=(tok_spec, weight_spec, weight_spec, weight_spec), check_vma=False)
```

profile of v0, /device:TPU:0, one launch (start us, length us, event | category | flops | bytes accessed | tf_op | source)
XLA Modules:
  0.0 1753.7 jit_solution(7245684207232205629)
XLA Ops:
  7.2 6.6 slice_bitcast_fusion.3
  18.8 7.1 fusion.95
  37.5 8.3 fusion.92
  56.4 6.6 fusion.94
  68.8 4.3 gather_fusion.31
  73.1 4.3 gather_fusion.30
  81.0 4.3 gather_fusion.19
  93.2 4.3 gather_fusion.25
  105.4 4.3 gather_fusion.13
  115.8 4.5 gather_fusion.1
  126.3 4.5 gather_fusion.7
  133.3 8.8 fusion.38
  142.1 4.8 fusion.32
  149.7 12.1 fusion.34
  161.8 10.3 fusion.28
  174.4 16.1 all_gather.14
  190.5 13.3 all_gather.13
  207.6 538.0 %all-reduce.3.cloned.1.call-done = (bf16[2,1024,2048]{2,1,0:T(8,128)(2,1)}, bf16[2,2048,1024]{2,1,0:T(8,128)(2,1)}, bf16[2,1024,2048]{2,1,0:T(8,128)(2,1)}, bf16...) async-done(((bf16[2,1024,2048]{2,1,0:T(8,128)(2,1)}, bf16[2,2048,1024]{2,1,0:T(8,128)(2,1)}, ...) | async-done | bytes 50331664 | tf_op jit(solution)/shard_map/psum | solution.py:66
  749.3 6.0 fusion.89
  757.9 4.3 gather_fusion.15
  768.9 6.0 fusion.91
  779.1 4.3 gather_fusion.33
  790.2 6.2 fusion.88
  796.4 4.3 gather_fusion.10
  811.6 6.3 fusion.90
  817.9 4.3 gather_fusion.28
  822.3 4.4 gather_fusion.27
  833.3 6.3 fusion.86
  854.8 6.3 fusion.87
  861.1 4.3 gather_fusion.4
  869.6 19.2 %fusion.33 = (bf16[2,1024,2048]{2,1,0:T(8,128)(2,1)}, bf16[2,1024,2048]{2,1,0:T(8,128)(2,1)}) fusion(bf16[2,1024,512]{2,1,0:T(8,128)(2,1)} %gather_fusion.17, bf16[2,1024,768]{2,1,0:T(8,128)(2,1)S(1)} %gather_fusion.16, bf16[2,1024,768]{2,1,0:T(8,128)(2,1)} %gather_fusion.15, pred[2]{0:T(512)(128)(4,1)S(1)} %get-tuple-element.87, ...), kind=kLoop, calls=%fused_computation.78 | loop fusion | flops 67108864 | bytes 50331656 | tf_op jit(solution)/shard_map/jit(_where)/select_n | solution.py:34
  888.8 26.5 %fusion.31 = (bf16[2,2048,1024]{2,1,0:T(8,128)(2,1)}, bf16[2,2048,1024]{2,1,0:T(8,128)(2,1)}) fusion(bf16[2,512,1024]{2,1,0:T(8,128)(2,1)} %gather_fusion.11, bf16[2,768,1024]{2,1,0:T(8,128)(2,1)} %gather_fusion.10, bf16[2,768,1024]{2,1,0:T(8,128)(2,1)} %gather_fusion.9, pred[2]{0:T(512)(128)(4,1)S(1)} %get-tuple-element.87, ...), kind=kLoop, calls=%fused_computation.74 | loop fusion | flops 67108864 | bytes 50331656 | tf_op jit(solution)/shard_map/jit(_where)/select_n | solution.py:34
  915.4 15.5 fusion.35
  930.9 43.8 %fusion.18 = f32[2,1024,4096]{2,1,0:T(8,128)} fusion(bf16[2,2048,1024]{2,1,0:T(8,128)(2,1)} %get-tuple-element.24, bf16[4096,2048]{1,0:T(8,128)(2,1)} %all-gather.3.cloned.1.call-done), kind=kOutput, calls=%fused_computation.61 | convolution fusion | flops 34359738368 | bytes 58720256 | tf_op jit(solution)/shard_map/nd,jdf->jnf/dot_general | solution.py:46
  974.6 52.8 %fusion.121 = bf16[2,4096,1024]{1,2,0:T(8,128)(2,1)} fusion(f32[2,1024,4096]{2,1,0:T(8,128)} %fusion.18, bf16[2,2048,1024]{2,1,0:T(8,128)(2,1)} %get-tuple-element.23, bf16[4096,2048]{1,0:T(8,128)(2,1)} %all-gather.3.cloned.1.call-done), kind=kOutput, calls=%fused_computation.48.clone.clone | convolution fusion | flops 34410070016 | bytes 75497472 | tf_op jit(solution)/shard_map/nd,jdf->jnf/dot_general | solution.py:45
  1027.4 61.6 %multiply_reduce_fusion.1 = f32[4096,2048]{1,0:T(8,128)} fusion(f32[2,4096]{1,0:T(2,128)S(1)} %copy-done.22, bf16[2,1024,2048]{2,1,0:T(8,128)(2,1)} %get-tuple-element.26, bf16[2,4096,1024]{1,2,0:T(8,128)(2,1)} %fusion.121), kind=kOutput, calls=%fused_computation.39 | convolution fusion | flops 34384904192 | bytes 58753024 | tf_op jit(solution)/shard_map/jnf,jfd->jnd/dot_general | solution.py:48
  1090.6 5.9 fusion.50
  1096.5 188.9 %reduce-scatter.3.cloned.1.call-done = f32[512,2048]{1,0:T(8,128)} async-done(((f32[4096,2048]{1,0:T(8,128)}), f32[512,2048]{1,0:T(8,128)}) %reduce-scatter.3.cloned.1.call-update) | async-done | bytes 4194320 | tf_op jit(solution)/shard_map/reduce_scatter | solution.py:50
  1285.4 11.2 add_convert_fusion.1
  1298.6 82.4 %all-gather.5.cloned.1.call-done = bf16[4096,2048]{1,0:T(8,128)(2,1)} async-done(((bf16[512,2048]{1,0:T(8,128)(2,1)}), bf16[4096,2048]{1,0:T(8,128)(2,1)}) %all-gather.5.cloned.1.call-update) | async-done | bytes 16777232 | tf_op jit(solution)/shard_map/all_gather | solution.py:38
  1380.9 43.9 %fusion.10 = f32[2,1024,4096]{2,1,0:T(8,128)} fusion(bf16[2,2048,1024]{2,1,0:T(8,128)(2,1)} %get-tuple-element.25, bf16[4096,2048]{1,0:T(8,128)(2,1)} %all-gather.5.cloned.1.call-done), kind=kOutput, calls=%fused_computation.57 | convolution fusion | flops 34359738368 | bytes 58720256 | tf_op jit(solution)/shard_map/nd,jdf->jnf/dot_general | solution.py:46
  1424.8 52.8 %fusion.117 = bf16[2,4096,1024]{1,2,0:T(8,128)(2,1)} fusion(f32[2,1024,4096]{2,1,0:T(8,128)} %fusion.10, bf16[2,2048,1024]{2,1,0:T(8,128)(2,1)} %get-tuple-element.22, bf16[4096,2048]{1,0:T(8,128)(2,1)} %all-gather.5.cloned.1.call-done), kind=kOutput, calls=%fused_computation.41.clone.clone.1 | convolution fusion | flops 34410070016 | bytes 75497472 | tf_op jit(solution)/shard_map/nd,jdf->jnf/dot_general | solution.py:45
  1477.6 61.6 %multiply_reduce_fusion = f32[4096,2048]{1,0:T(8,128)} fusion(f32[2,4096]{1,0:T(2,128)S(1)} %copy-done.23, bf16[2,1024,2048]{2,1,0:T(8,128)(2,1)} %get-tuple-element.27, bf16[2,4096,1024]{1,2,0:T(8,128)(2,1)} %fusion.117), kind=kOutput, calls=%fused_computation.38 | convolution fusion | flops 34384904192 | bytes 58753024 | tf_op jit(solution)/shard_map/jnf,jfd->jnd/dot_general | solution.py:48
  1539.3 16.7 pad_maximum_fusion
  1556.0 8.3 pad_maximum_fusion.1
  1567.5 8.0 pad_maximum_fusion.2
  1579.3 156.3 %reduce-scatter.5.cloned.1.call-done = f32[512,2048]{1,0:T(8,128)} async-done(((f32[4096,2048]{1,0:T(8,128)}), f32[512,2048]{1,0:T(8,128)}) %reduce-scatter.5.cloned.1.call-update) | async-done | bytes 4194320 | tf_op jit(solution)/shard_map/reduce_scatter | solution.py:50
  1735.6 11.1 add_convert_fusion
  (196 shorter events, 147.1 us)
Async XLA Ops:
  7.2 738.4 %all-reduce.3.cloned.1.call-start = ((), (), s32[]{:S(2)}) async-start(), calls=%async_computation.6 | async-start | bytes 100663296 | tf_op jit(solution)/shard_map/psum | solution.py:66
  17.2 10.3 slice-start.4
  18.8 8.7 slice-start.5
  18.8 10.0 slice-start.6
  18.8 11.2 slice-start.7
  34.2 13.1 slice-start
  37.5 9.9 slice-start.1
  37.5 10.0 slice-start.2
  37.5 11.6 slice-start.3
  64.6 8.5 copy-start
  133.3 8.8 copy-start.13
  133.3 8.8 copy-start.14
  133.3 8.8 copy-start.15
  142.1 4.8 copy-start.5
  142.1 5.7 copy-start.6
  142.1 6.6 copy-start.7
  142.1 7.5 copy-start.8
  149.6 12.1 copy-start.9
  149.6 12.1 copy-start.10
  149.6 12.1 copy-start.11
  149.6 12.1 copy-start.12
  172.1 18.4 %copy-start.21 = (s32[2,512,8]{1,2,0:T(8,128)S(1)}, s32[2,512,8]{1,2,0:T(8,128)}, u32[]{:S(2)}) copy-start(s32[2,512,8]{1,2,0:T(8,128)} %param.17) | copy-start | bytes 98308
  172.1 758.8 %all-gather.3.cloned.1.call-start = ((), (), s32[]{:S(2)}) async-start(), calls=%async_computation.2 | async-start | bytes 18874368 | tf_op jit(solution)/shard_map/all_gather | solution.py:38
  172.8 1112.6 %reduce-scatter.3.cloned.1.call-start = ((), (), s32[]{:S(2)}) async-start(), calls=%async_computation.3 | async-start | bytes 37748736 | tf_op jit(solution)/shard_map/reduce_scatter | solution.py:50
  869.6 45.7 %slice-start.8 = ((s8[16777216]{0:T(1024)(128)(4,1)}), s8[4194304]{0:T(1024)(128)(4,1)S(1)}, s32[]{:S(2)}) async-start(s8[16777216]{0:T(1024)(128)(4,1)} %bitcast.181), calls=%async_computation.15 | async-start | bytes 8388608
  869.6 45.7 %slice-start.9 = ((s8[16777216]{0:T(1024)(128)(4,1)}), s8[4194304]{0:T(1024)(128)(4,1)S(1)}, s32[]{:S(2)}) async-start(s8[16777216]{0:T(1024)(128)(4,1)} %bitcast.181), calls=%async_computation.16 | async-start | bytes 8388608
  888.8 26.5 %slice-start.10 = ((s8[16777216]{0:T(1024)(128)(4,1)}), s8[4194304]{0:T(1024)(128)(4,1)S(1)}, s32[]{:S(2)}) async-start(s8[16777216]{0:T(1024)(128)(4,1)} %bitcast.181), calls=%async_computation.17 | async-start | bytes 8388608
  888.8 26.5 %slice-start.11 = ((s8[16777216]{0:T(1024)(128)(4,1)}), s8[4194304]{0:T(1024)(128)(4,1)S(1)}, s32[]{:S(2)}) async-start(s8[16777216]{0:T(1024)(128)(4,1)} %bitcast.181), calls=%async_computation.18 | async-start | bytes 8388608
  974.6 52.8 %copy-start.22 = (f32[2,4096]{1,0:T(2,128)S(1)}, f32[2,4096]{1,0:T(2,128)}, u32[]{:S(2)}) copy-start(f32[2,4096]{1,0:T(2,128)} %multiply_bitcast_fusion.1) | copy-start | bytes 98308
  1089.0 291.9 %all-gather.5.cloned.1.call-start = ((), (), s32[]{:S(2)}) async-start(), calls=%async_computation.4 | async-start | bytes 18874368 | tf_op jit(solution)/shard_map/all_gather | solution.py:38
  1096.5 200.3 %copy-start.1 = (s32[16]{0:T(128)S(1)}, s32[16]{0:T(128)}, u32[]{:S(2)}) copy-start(s32[16]{0:T(128)} %copy-done) | copy-start | bytes 196
  1096.5 200.3 %copy-start.25 = (s32[2]{0:T(128)S(1)}, s32[2]{0:T(128)}, u32[]{:S(2)}) copy-start(s32[2]{0:T(128)} %copy-done.24) | copy-start | bytes 28
  1096.5 200.3 %copy-start.27 = (s32[2]{0:T(128)S(1)}, s32[2]{0:T(128)}, u32[]{:S(2)}) copy-start(s32[2]{0:T(128)} %get-tuple-element.63) | copy-start | bytes 28
  1096.5 201.2 %copy-start.18 = (f32[4096,8]{0,1:T(8,128)S(1)}, f32[4096,8]{0,1:T(8,128)}, u32[]{:S(2)}) copy-start(f32[4096,8]{0,1:T(8,128)} %get-tuple-element.61) | copy-start | bytes 393220
  1096.5 201.2 %copy-start.19 = (s32[4096,8]{0,1:T(8,128)S(1)}, s32[4096,8]{0,1:T(8,128)}, u32[]{:S(2)}) copy-start(s32[4096,8]{0,1:T(8,128)} %get-tuple-element.59) | copy-start | bytes 393220
  1296.7 438.9 %reduce-scatter.5.cloned.1.call-start = ((), (), s32[]{:S(2)}) async-start(), calls=%async_computation.5 | async-start | bytes 37748736 | tf_op jit(solution)/shard_map/reduce_scatter | solution.py:50
  1424.8 52.8 %copy-start.23 = (f32[2,4096]{1,0:T(2,128)S(1)}, f32[2,4096]{1,0:T(2,128)}, u32[]{:S(2)}) copy-start(f32[2,4096]{1,0:T(2,128)} %multiply_bitcast_fusion) | copy-start | bytes 98308
  1539.2 16.7 slice-start.16
  1539.2 16.7 slice-start.18
  1539.2 16.7 slice-start.17
  1539.2 16.7 slice-start.19
  1555.9 8.4 slice-start.12
  1555.9 8.5 slice-start.14
  1556.0 10.3 slice-start.13
  1556.0 11.5 slice-start.15
  1556.0 19.5 %slice-start.20 = ((s8[8388608]{0:T(1024)(128)(4,1)}), s8[4194304]{0:T(1024)(128)(4,1)S(1)}, s32[]{:S(2)}) async-start(s8[8388608]{0:T(1024)(128)(4,1)} %bitcast.197), calls=%async_computation.27 | async-start | bytes 8388608
  1564.4 11.2 slice-start.21
  1567.5 8.1 copy-start.17
  (9 other events, 20.7 us)
Sparse Core Ops, SparseCore 0:
  172.2 573.3 all-reduce.2
  747.4 84.0 all-gather.2
  1089.2 196.2 reduce-scatter.2
  1296.8 84.0 all-gather.4
  1539.3 196.1 reduce-scatter.4
where the time goes:
time: 1760 us; the launch traced here: 1750 us
  waiting for transfers between devices  966 us (55%)
  matrix products  348 us (20%)
  local copies, waits for them, and re-layouts  260 us (15%)
  other arithmetic  135 us (8%)
  blocking collectives  29.4 us (2%)
    psum x1, waiting for transfers between devices, body(): arrived = lax.psum(outgoing, 'ep')  538 us
    reduce_scatter x2, waiting for transfers between devices, moe_layer(): lax.psum_scatter(partial_sum, 'ep', scatter_dimension=0, tiled=True)  345 us
    gather x30, local copies, waits for them, and re-layouts, place_moved(): jnp.take(arrived_arr, pick_idx, axis=0)  124 us
    dot_general x2, matrix products, moe_layer(): jnp.einsum('jnf,jfd->jnd', inner_act, expert_w[2], preferred_element_type...  123 us
    dot_general x2, matrix products, moe_layer(): jnp.einsum('nd,jdf->jnf', gathered, expert_w[0], preferred_element_type=j...  106 us
    gather x27, local copies, waits for them, and re-layouts, send_moved(): jnp.take(weight_arr, local_idx, axis=0)  103 us
    dot_general x2, matrix products, moe_layer(): jnp.einsum('nd,jdf->jnf', gathered, expert_w[1], preferred_element_type=j...  87.7 us
    all_gather x2, waiting for transfers between devices, moe_layer(): gathered = lax.all_gather(hidden, 'ep', axis=0, tiled=True)  82.4 us
  transfers between devices with their start and end apart: 5, of which 4 were waited for; matrix products, arithmetic and copies ran while one was open for 13% of the time, Pallas kernels for 0%

commit v1 on v0

v1 whole, which is shorter than its diff:
```python
import functools

import jax
import jax.numpy as jnp
from jax import lax
from jax.experimental import pallas as pl
from jax.experimental.pallas import tpu as pltpu
from jax.sharding import PartitionSpec as P

TOKEN_AXES = ('replica', 'ep')
MESH = pl.DeviceIdType.MESH
F_TILE = 512
N_TILE = 1024


def first_holder(slot_map, wanted):
    slot_ids = jnp.arange(slot_map.shape[0], dtype=jnp.int32)
    hit_mask = slot_map[None, :] == wanted[:, None]
    return jnp.min(jnp.where(hit_mask, slot_ids[None, :], slot_map.shape[0]), axis=1)


def send_moved(weights, slot_map, move_expert, slots_dev, my_dev):
    source = first_holder(slot_map, move_expert)
    is_source = (source // slots_dev) == my_dev
    local_idx = source % slots_dev
    return tuple(jnp.where(is_source[:, None, None], jnp.take(weight_arr, local_idx, axis=0), jnp.zeros((), weight_arr.dtype)) for weight_arr in weights)


def place_moved(weights, arrived, move_slot, slots_dev, my_dev):
    local_ids = my_dev * slots_dev + jnp.arange(slots_dev, dtype=jnp.int32)
    match_mask = (move_slot[None, :] == local_ids[:, None]).astype(jnp.int32)
    is_target = jnp.max(match_mask, axis=1) > 0
    pick_idx = jnp.argmax(match_mask, axis=1)
    return tuple(jnp.where(is_target[:, None, None], jnp.take(arrived_arr, pick_idx, axis=0), weight_arr) for arrived_arr, weight_arr in zip(arrived, weights))


def slot_coefs(routes, gates, slot_map, slots_dev, my_dev):
    slot_ids = jnp.arange(slot_map.shape[0], dtype=jnp.int32)
    serve = (first_holder(slot_map, slot_map) == slot_ids).astype(jnp.float32)
    hit_mask = routes[:, :, None] == slot_map[None, None, :]
    coef = jnp.sum(jnp.where(hit_mask, gates[:, :, None], 0.0), axis=1) * serve[None, :]
    coef = coef.T.reshape(-1, 2, slots_dev, routes.shape[0])
    core = my_dev % 2
    coef = jnp.where(core == 0, coef, coef[:, ::-1])
    coef = coef.reshape(coef.shape[0], 2 * slots_dev, routes.shape[0])
    return jnp.pad(coef, ((0, 0), (0, 8 - 2 * slots_dev), (0, 0)))


def layer_kernel(layer, h_ref, ct_ref, wg_ref, wu_ref, wd_ref, sg_ref, su_ref, sd_ref,
                 out_ref, xg_ref, pout_ref, hs_ref, rcv_ref,
                 wg_v, wu_v, wd_v, xbuf, pbuf, ab, obuf, cbuf, ccol, send_sem, recv_sem, loc_sem):
    me = lax.axis_index('ep')
    core = me % 2
    x = (me // 2) % 2
    y = me // 4
    chip = me // 2
    to_core = me + 1 - 2 * core
    to_x = me + 2 - 4 * x
    to_y = me + 4 - 8 * y
    to_d = me + 6 - 4 * x - 8 * y
    rows = xbuf.shape[0]
    half = rows // 2

    def remote(i, src, dst, dev):
        return pltpu.make_async_remote_copy(src_ref=src, dst_ref=dst, send_sem=send_sem.at[i], recv_sem=recv_sem.at[i], device_id={'ep': dev}, device_id_type=MESH)

    def local(i, src, dst):
        return pltpu.make_async_copy(src, dst, loc_sem.at[i])

    own_a, own_b = h_ref.at[pl.ds(0, rows)], h_ref.at[pl.ds(rows, rows)]
    lo, hi = pl.ds(0, half), pl.ds(half, half)
    ag = [
        remote(0, own_a, xg_ref.at[0], to_x),
        remote(1, own_b, xg_ref.at[1], to_y),
        remote(2, xg_ref.at[0], xg_ref.at[2], to_y),
        remote(3, xg_ref.at[1], xg_ref.at[3], to_x),
        remote(4, own_b, xg_ref.at[4], to_x),
        remote(5, own_a, xg_ref.at[5], to_y),
    ]
    cs = [
        remote(6, ct_ref.at[(chip + 1 - 2 * x)], cbuf.at[1], to_x),
        remote(7, ct_ref.at[(chip + 2 - 4 * y)], cbuf.at[2], to_y),
        remote(8, ct_ref.at[(chip + 3 - 2 * x - 4 * y)], cbuf.at[3], to_d),
    ]
    ws = [
        remote(9, wg_ref.at[layer], wg_v.at[pl.ds(2, 2)], to_core),
        remote(10, wu_ref.at[layer], wu_v.at[pl.ds(2, 2)], to_core),
        remote(11, wd_ref.at[layer], wd_v.at[pl.ds(2, 2)], to_core),
    ]
    s_xa = remote(12, pout_ref.at[0], rcv_ref.at[0], to_x)
    s_da = [remote(13, pout_ref.at[2, lo], rcv_ref.at[1, lo], to_x), remote(14, pout_ref.at[2, hi], rcv_ref.at[1, hi], to_x)]
    s_yb = remote(15, pout_ref.at[1], rcv_ref.at[2], to_y)
    s_db = [remote(16, pout_ref.at[3, lo], rcv_ref.at[3, lo], to_y), remote(17, pout_ref.at[3, hi], rcv_ref.at[3, hi], to_y)]
    s_xb = [remote(18, pout_ref.at[4, lo], rcv_ref.at[4, lo], to_x), remote(19, pout_ref.at[4, hi], rcv_ref.at[4, hi], to_x)]
    s_ya = [remote(20, pout_ref.at[5, lo], rcv_ref.at[5, lo], to_y), remote(21, pout_ref.at[5, hi], rcv_ref.at[5, hi], to_y)]

    barrier = pltpu.get_barrier_semaphore()
    for dev in (to_core, to_x, to_y, to_d):
        pl.semaphore_signal(barrier, inc=1, device_id={'ep': dev}, device_id_type=MESH)
    pl.semaphore_wait(barrier, 4)

    for c in cs:
        c.start()
    for i in (0, 1, 4, 5):
        ag[i].start()
    for c in ws:
        c.start()

    shared_in = [local(0, sg_ref.at[layer], wg_v.at[1]), local(1, su_ref.at[layer], wu_v.at[1]), local(2, sd_ref.at[layer], wd_v.at[1])]
    first_in = [local(3, wg_ref.at[layer, 0], wg_v.at[0]), local(4, wu_ref.at[layer, 0], wu_v.at[0]), local(5, wd_ref.at[layer, 0], wd_v.at[0])]
    second_in = [local(0, wg_ref.at[layer, 1], wg_v.at[1]), local(1, wu_ref.at[layer, 1], wu_v.at[1]), local(2, wd_ref.at[layer, 1], wd_v.at[1])]
    coef_in = local(6, ct_ref.at[chip], cbuf.at[0])
    for c in shared_in:
        c.start()
    for c in first_in:
        c.start()
    coef_in.start()

    def expert(slot, acc, coef):
        def f_step(ft, carry):
            cols = pl.ds(pl.multiple_of(ft * F_TILE, F_TILE), F_TILE)
            tok = xbuf[...]
            gate_proj = jnp.dot(tok, wg_v[slot, :, cols], preferred_element_type=jnp.float32)
            up_proj = jnp.dot(tok, wu_v[slot, :, cols], preferred_element_type=jnp.float32)
            inner = (jax.nn.silu(gate_proj) * up_proj).astype(jnp.bfloat16)
            for n in range(acc.shape[1] // N_TILE):
                ns = pl.ds(n * N_TILE, N_TILE)
                part = jnp.dot(inner, wd_v[slot, cols, ns], preferred_element_type=jnp.float32)
                acc[:, ns] += part if coef is None else coef * part
            return carry
        lax.fori_loop(0, wg_v.shape[2] // F_TILE, f_step, 0)

    for c in shared_in:
        c.wait()

    def shared_step(p, carry):
        src = h_ref.at[pl.ds(pl.multiple_of(p * rows, rows), rows)]
        load = local(7, src, xbuf)
        load.start()
        load.wait()
        acc = pbuf.at[0]
        acc[...] = xbuf[...].astype(jnp.float32)
        expert(1, acc, None)
        store = local(7, acc, hs_ref.at[p])
        store.start()
        store.wait()
        return carry
    lax.fori_loop(0, 2, shared_step, 0)
    for c in second_in:
        c.start()

    ag[0].wait_recv()
    ag[2].start()
    ag[1].wait_recv()
    ag[3].start()

    for c in cs:
        c.wait_recv()
    coef_in.wait()
    for k, (rel, part) in enumerate([(1, 0), (2, 1), (3, 0), (3, 1), (1, 1), (2, 0), (0, 0), (0, 1)]):
        ccol[k, :, pl.ds(0, 8)] = jnp.transpose(cbuf[rel, :, pl.ds(part * rows, rows)])
    for c in second_in + first_in:
        c.wait()
    for c in ws:
        c.wait_recv()

    def add_half(h):
        part = lo if h == 0 else hi
        for mine, theirs, arrived, out in ((4, 3, s_db[h], s_xb[h]), (5, 1, s_da[h], s_ya[h])):
            load_a = local(0, pout_ref.at[mine, part], ab.at[0])
            load_a.start()
            arrived.wait_recv()
            load_b = local(1, rcv_ref.at[theirs, part], ab.at[1])
            load_b.start()
            load_a.wait()
            load_b.wait()
            ab[0] = ab[0] + ab[1]
            store = local(0, ab.at[0], pout_ref.at[mine, part])
            store.start()
            store.wait()
            out.start()

    def step(k, carry):
        for j in range(2, 6):
            @pl.when(k == j)
            def _():
                ag[j].wait_recv()
        acc = pbuf.at[k % 2]

        @pl.when(k < 6)
        def _():
            load = local(7, xg_ref.at[lax.rem(k, 6)], xbuf)
            load.start()
            acc[...] = jnp.zeros_like(acc)
            load.wait()

        @pl.when(k >= 6)
        def _():
            p = k % 2
            load = local(7, h_ref.at[pl.ds(pl.multiple_of(p * rows, rows), rows)], xbuf)
            load_s = local(6, hs_ref.at[p], acc)
            load.start()
            load_s.start()
            load.wait()
            load_s.wait()

        def slot_step(slot, c):
            coefs = ccol[k, :, pl.ds(0, 8)]
            lane = lax.broadcasted_iota(jnp.int32, coefs.shape, 1)
            col = jnp.sum(jnp.where(lane == slot, coefs, 0.0), axis=1, keepdims=True)
            expert(slot, acc, col)
            return c
        lax.fori_loop(0, wg_v.shape[0], slot_step, 0)

        @pl.when(k < 6)
        def _():
            store = local(7, acc, pout_ref.at[lax.rem(k, 6)])
            store.start()
            store.wait()
        for j, outs in ((0, [s_xa]), (1, [s_yb]), (2, s_da), (3, s_db)):
            @pl.when(k == j)
            def _():
                for c in outs:
                    c.start()
        for j, h in ((5, 0), (6, 1)):
            @pl.when(k == j)
            def _():
                add_half(h)
        return carry
    lax.fori_loop(0, 8, step, 0)

    s_xa.wait_recv()
    s_yb.wait_recv()
    for h, part in enumerate((lo, hi)):
        loads = [local(0, rcv_ref.at[0, part], ab.at[0]), local(1, rcv_ref.at[2, part], ab.at[1])]
        for c in loads:
            c.start()
        for i, c in enumerate(loads):
            c.wait()
            pbuf[i, part] = pbuf[i, part] + ab[i]
    stores = []
    for h, part in enumerate((lo, hi)):
        loads = []
        for i, (arrived, src) in enumerate(((s_ya[h], 5), (s_xb[h], 4))):
            arrived.wait_recv()
            load = local(i, rcv_ref.at[src, part], ab.at[i])
            load.start()
            loads.append(load)
        for i, c in enumerate(loads):
            c.wait()
            obuf[2 * h + i] = (pbuf[i, part] + ab[i]).astype(jnp.bfloat16)
            store = local(2 + 2 * h + i, obuf.at[2 * h + i], out_ref.at[pl.ds(i * rows + h * half, half)])
            store.start()
            stores.append(store)
    for c in stores:
        c.wait()
    for c in ag + cs + ws + [s_xa, s_yb] + s_da + s_db + s_xb + s_ya:
        c.wait_send()


def moe_layer(layer, hidden, coefs, weights, shared):
    tokens, width = hidden.shape
    inner = weights[0].shape[3]
    rows = tokens // 2
    f32, bf16 = jnp.float32, jnp.bfloat16
    any_spec = pl.BlockSpec(memory_space=pl.ANY)
    flops = 2 * 3 * width * inner * (4 * 4 * tokens + tokens)
    outs = pl.pallas_call(
        functools.partial(layer_kernel, layer),
        out_shape=(
            jax.ShapeDtypeStruct((tokens, width), bf16),
            jax.ShapeDtypeStruct((6, rows, width), bf16),
            jax.ShapeDtypeStruct((6, rows, width), f32),
            jax.ShapeDtypeStruct((2, rows, width), f32),
            jax.ShapeDtypeStruct((6, rows, width), f32),
        ),
        in_specs=[any_spec] * 8,
        out_specs=[any_spec] * 5,
        scratch_shapes=[
            pltpu.VMEM((4, width, inner), bf16),
            pltpu.VMEM((4, width, inner), bf16),
            pltpu.VMEM((4, inner, width), bf16),
            pltpu.VMEM((rows, width), bf16),
            pltpu.VMEM((2, rows, width), f32),
            pltpu.VMEM((2, rows // 2, width), f32),
            pltpu.VMEM((4, rows // 2, width), bf16),
            pltpu.VMEM((4, 8, tokens), f32),
            pltpu.VMEM((8, rows, 128), f32),
            pltpu.SemaphoreType.DMA((22,)),
            pltpu.SemaphoreType.DMA((22,)),
            pltpu.SemaphoreType.DMA((8,)),
        ],
        compiler_params=pltpu.CompilerParams(collective_id=layer, has_side_effects=True, vmem_limit_bytes=67043328),
        cost_estimate=pl.CostEstimate(flops=flops, bytes_accessed=200 * 2 ** 20, transcendentals=0),
        name=f'moe_layer_{layer}',
    )(hidden, coefs, *weights, *shared)
    return outs[0]


def solution(mesh):
    def body(tok_in, routes, gate_vals, w_gate, w_up, w_down, sh_gate, sh_up, sh_down, old_map, move_slot, move_expert):
        my_dev = lax.axis_index('ep')
        slots_dev = w_gate.shape[1]
        hidden = tok_in
        placed = []
        for layer_idx in range(2):
            layer_w = (w_gate[layer_idx], w_up[layer_idx], w_down[layer_idx])
            outgoing = send_moved(layer_w, old_map[layer_idx], move_expert[layer_idx], slots_dev, my_dev)
            arrived = lax.psum(outgoing, 'ep')
            placed.append(place_moved(layer_w, arrived, move_slot[layer_idx], slots_dev, my_dev))
        for layer_idx in range(2):
            coefs = slot_coefs(routes[layer_idx], gate_vals[layer_idx], old_map[layer_idx], slots_dev, my_dev)
            hidden = moe_layer(layer_idx, hidden, coefs, (w_gate, w_up, w_down), (sh_gate, sh_up, sh_down))
        new_gate = jnp.stack([placed[0][0], placed[1][0]])
        new_up = jnp.stack([placed[0][1], placed[1][1]])
        new_down = jnp.stack([placed[0][2], placed[1][2]])
        return (hidden, new_gate, new_up, new_down)

    weight_spec = P(None, TOKEN_AXES, None, None)
    route_spec = P(None, TOKEN_AXES, None)
    map_spec = P(None, 'replica')
    shared_spec = P(None, None, None)
    tok_spec = P(TOKEN_AXES, None)
    return jax.shard_map(body, mesh=mesh, in_specs=(tok_spec, route_spec, route_spec, weight_spec, weight_spec, weight_spec, shared_spec, shared_spec, shared_spec, map_spec, map_spec, map_spec), out_specs=(tok_spec, weight_spec, weight_spec, weight_spec), check_vma=False)
```

time: 1760 us -> 1340 us (0.76)
  waiting for transfers between devices: 966 us -> 147 us
  Pallas kernels: 0 us -> 808 us
  matrix products: 348 us -> 0 us
  blocking collectives: 29.4 us -> 0 us
  local copies, waits for them, and re-layouts: 260 us -> 239 us
    pallas_call x0 -> x2, Pallas kernels: none -> 808 us  [moe_layer(): pl.pallas_call(functools.partial(layer_kernel, layer), out_shape=(jax.Sha...]
    psum x1, waiting for transfers between devices: 538 us -> 147 us  [body(): arrived = lax.psum(outgoing, 'ep')]
    dot_general x10 -> x0, matrix products: 348 us -> none  [the longest x2 123 us: moe_layer(): jnp.einsum('jnf,jfd->jnd', inner_act, expert_w[2], preferred_element_type...]
    reduce_scatter x2 -> x0, waiting for transfers between devices: 345 us -> none  [moe_layer(): lax.psum_scatter(partial_sum, 'ep', scatter_dimension=0, tiled=True)]
    all_gather x2 -> x0, waiting for transfers between devices: 82.4 us -> none  [moe_layer(): gathered = lax.all_gather(hidden, 'ep', axis=0, tiled=True)]
    select_n x4 -> x2, other arithmetic: 61.7 us -> 0.03 us  [slot_coefs(): coef = jnp.where(core == 0, coef, coef[:, ::-1])]
    all_gather x2 -> x0, blocking collectives: 29.4 us -> none  [the longest x1 16.1 us: body(): gate_all = lax.all_gather(gate_vals, 'ep', axis=1, tiled=True)]
    another operation x1 -> x2, other arithmetic: 8.02 us -> 32.7 us  [body(): new_down = jnp.stack([placed[0][2], placed[1][2]])]
  transfers between devices with their start and end apart: 5 -> 1, of which waited for: 4 -> 1; matrix products, arithmetic and copies ran while one was open for 13% -> 0% of each run, Pallas kernels for 0% -> 61%
where the time goes in v1:
time: 1340 us; the launch traced here: 1330 us
  Pallas kernels  808 us (60%)
  local copies, waits for them, and re-layouts  239 us (18%)
  waiting for transfers between devices  147 us (11%)
  other arithmetic  119 us (9%)
  between operations  14.8 us (1%)
    pallas_call x2, Pallas kernels, moe_layer(): pl.pallas_call(functools.partial(layer_kernel, layer), out_shape=(jax.Sha...  808 us
    psum x1, waiting for transfers between devices, body(): arrived = lax.psum(outgoing, 'ep')  147 us
    gather x30, local copies, waits for them, and re-layouts, place_moved(): jnp.take(arrived_arr, pick_idx, axis=0)  107 us
    gather x27, local copies, waits for them, and re-layouts, send_moved(): jnp.take(weight_arr, local_idx, axis=0)  99.1 us
    select_n x4, other arithmetic, send_moved(): jnp.where(is_source[:, None, None], jnp.take(weight_arr, local_idx, axis=...  35.3 us
    another operation x2, other arithmetic, body(): new_down = jnp.stack([placed[0][2], placed[1][2]])  32.7 us
    another operation x2, other arithmetic, body(): new_up = jnp.stack([placed[0][1], placed[1][1]])  29.8 us
  transfers between devices with their start and end apart: 1, of which 1 were waited for; matrix products, arithmetic and copies ran while one was open for 0% of the time, Pallas kernels for 61%

profile of v1, /device:TPU:0, one launch (start us, length us, event | category | flops | bytes accessed | tf_op | source)
XLA Modules:
  0.0 1327.1 jit_solution(13835975101059958851)
XLA Ops:
  7.2 6.9 slice_bitcast_fusion.5
  19.0 7.2 fusion.36
  30.2 4.2 slice_bitcast_fusion.3
  37.7 8.3 fusion.34
  49.3 4.2 slice_bitcast_fusion.1
  56.6 6.5 fusion.32
  64.9 4.3 gather_fusion
  69.2 4.3 gather_fusion.1
  73.5 4.4 gather_fusion.12
  77.9 4.3 gather_fusion.13
  82.1 3.6 gather_fusion.2
  89.3 4.3 gather_fusion.6
  96.0 4.4 gather_fusion.18
  102.9 3.8 gather_fusion.8
  108.7 4.4 gather_fusion.24
  119.1 4.4 gather_fusion.30
  125.9 3.8 gather_fusion.32
  129.8 8.3 fusion.12
  138.2 4.8 fusion.15
  145.7 12.1 fusion.6
  157.8 10.1 fusion.9
  170.4 413.7 %moe_layer_0.1 = (bf16[512,2048]{1,0:T(8,128)(2,1)}, bf16[6,256,2048]{2,1,0:T(8,128)(2,1)}, f32[6,256,2048]{2,1,0:T(8,128)}, f32[2,256,2048]{2,1,0:T(8,128)}, f32[6,256,2048]{2,1,0:T(8,128)}) custom-call(bf16[512,2048]{1,0:T(8,128)(2,1)} %h_ref.1, f32[4,8,512]{2,1,0:T(8,128)} %pad.7.ct_ref, bf16[2,2,2048,1024]{3,2,1,0:T(8,128)(2,1)} %wg_ref.3, ...), custom_call_target="tpu_custom_call" | custom-call | flops 109521666048 | bytes 209715200 | tf_op jit(solution)/shard_map/moe_layer_0/pallas_call | solution.py:268
  584.2 393.9 %moe_layer_1.1 = (bf16[512,2048]{1,0:T(8,128)(2,1)}, bf16[6,256,2048]{2,1,0:T(8,128)(2,1)}, f32[6,256,2048]{2,1,0:T(8,128)}, f32[2,256,2048]{2,1,0:T(8,128)}, f32[6,256,2048]{2,1,0:T(8,128)}) custom-call(bf16[512,2048]{1,0:T(8,128)(2,1)} %get-tuple-element.10.h_ref, f32[4,8,512]{2,1,0:T(8,128)} %pad.8.ct_ref, bf16[2,2,2048,1024]{3,2,1,0:T(8,128)(2,1)} %wg_ref.3, ...), custom_call_target="tpu_custom_call" | custom-call | flops 109521666048 | bytes 209715200 | tf_op jit(solution)/shard_map/moe_layer_1/pallas_call | solution.py:268
  980.7 146.6 %all-reduce.5.cloned.1.call-done = (bf16[2,2048,1024]{2,1,0:T(8,128)(2,1)}, bf16[2,2048,1024]{2,1,0:T(8,128)(2,1)}, bf16[2,2048,1024]{2,1,0:T(8,128)(2,1)}, bf16...) async-done(((bf16[2,2048,1024]{2,1,0:T(8,128)(2,1)}, bf16[2,2048,1024]{2,1,0:T(8,128)(2,1)}, ...) | async-done | bytes 50331664 | tf_op jit(solution)/shard_map/psum | solution.py:309
  1127.3 6.6 fusion.26
  1137.0 3.7 fusion.27
  1148.5 3.9 fusion.29
  1167.7 4.3 gather_fusion.28
  1172.0 4.3 gather_fusion.33
  1176.3 4.4 gather_fusion.34
  1184.3 3.6 gather_fusion.35
  1187.9 4.3 gather_fusion.15
  1192.2 4.3 gather_fusion.16
  1196.5 4.3 gather_fusion.21
  1200.8 4.2 gather_fusion.22
  1205.1 3.6 gather_fusion.17
  1208.7 3.6 gather_fusion.23
  1212.3 4.3 gather_fusion.3
  1216.6 4.3 gather_fusion.4
  1220.9 4.4 gather_fusion.9
  1225.3 4.3 gather_fusion.10
  1233.2 3.6 gather_fusion.5
  1236.8 18.7 %fusion.14 = (bf16[1,2,1024,2048]{3,2,1,0:T(8,128)(2,1)}, bf16[1,2,1024,2048]{3,2,1,0:T(8,128)(2,1)}) fusion(bf16[2,1024,512]{2,1,0:T(8,128)(2,1)} %gather_fusion.29, bf16[2,1024,768]{2,1,0:T(8,128)(2,1)} %gather_fusion.28, bf16[2,1024,768]{2,1,0:T(8,128)(2,1)S(1)} %gather_fusion.27, pred[2]{0:T(512)(128)(4,1)S(1)} %get-tuple-element.93, ...), kind=kLoop, calls=%fused_computation.63 | loop fusion | flops 67108864 | bytes 50331656 | tf_op jit(solution)/shard_map/stack | solution.py:316
  1255.5 14.0 %pad_maximum_fusion.2 = bf16[2,2,1024,2048]{3,2,1,0:T(8,128)(2,1)} fusion(bf16[1,2,1024,2048]{3,2,1,0:T(8,128)(2,1)} %get-tuple-element.27, bf16[1,2,1024,2048]{3,2,1,0:T(8,128)(2,1)} %get-tuple-element.26), kind=kLoop, calls=%fused_computation.38 | loop fusion | flops 8388608 | bytes 33554432 | tf_op jit(solution)/shard_map/stack | solution.py:316
  1269.6 16.0 %fusion.8 = (bf16[1,2,2048,1024]{3,2,1,0:T(8,128)(2,1)}, bf16[1,2,2048,1024]{3,2,1,0:T(8,128)(2,1)}) fusion(bf16[2,512,1024]{2,1,0:T(8,128)(2,1)} %gather_fusion.17, bf16[2,768,1024]{2,1,0:T(8,128)(2,1)} %gather_fusion.16, bf16[2,768,1024]{2,1,0:T(8,128)(2,1)} %gather_fusion.15, pred[2]{0:T(512)(128)(4,1)S(1)} %get-tuple-element.93, ...), kind=kLoop, calls=%fused_computation.53 | loop fusion | flops 67108864 | bytes 50331656 | tf_op jit(solution)/shard_map/stack | solution.py:315
  1285.5 13.8 %pad_maximum_fusion.1 = bf16[2,2,2048,1024]{3,2,1,0:T(8,128)(2,1)} fusion(bf16[1,2,2048,1024]{3,2,1,0:T(8,128)(2,1)} %get-tuple-element.29, bf16[1,2,2048,1024]{3,2,1,0:T(8,128)(2,1)} %get-tuple-element.28), kind=kLoop, calls=%fused_computation.37 | loop fusion | flops 8388608 | bytes 33554432 | tf_op jit(solution)/shard_map/stack | solution.py:315
  1299.3 12.4 fusion.2
  1311.7 6.8 pad_maximum_fusion
  (158 shorter events, 81.6 us)
Async XLA Ops:
  7.2 1120.1 %all-reduce.5.cloned.1.call-start = ((), (), s32[]{:S(2)}) async-start(), calls=%async_computation | async-start | bytes 100663296 | tf_op jit(solution)/shard_map/psum | solution.py:309
  14.1 3.4 copy-start
  17.5 10.2 slice-start.4
  19.0 8.7 slice-start.5
  19.0 10.0 slice-start.6
  19.0 11.2 slice-start.7
  34.4 13.1 slice-start
  37.7 9.8 slice-start.1
  37.7 10.0 slice-start.2
  37.7 11.6 slice-start.3
  63.1 1.6 copy-start.20
  63.1 1.6 copy-start.21
  96.0 4.5 copy-start.2
  102.9 3.8 copy-start.16
  108.7 4.5 copy-start.3
  119.1 4.4 copy-start.1
  125.9 3.8 copy-start.12
  129.8 8.3 copy-start.13
  129.8 8.3 copy-start.14
  129.8 8.3 copy-start.15
  138.1 4.8 copy-start.4
  138.1 5.7 copy-start.5
  138.1 6.6 copy-start.6
  138.1 7.5 copy-start.7
  145.7 12.1 copy-start.8
  145.7 12.1 copy-start.9
  145.7 12.1 copy-start.10
  145.7 12.1 copy-start.11
  167.9 0.8 copy-start.18
  167.9 0.8 copy-start.19
  1127.3 9.7 slice-start.20
  1127.3 9.7 slice-start.21
  1136.9 5.3 slice-start.18
  1136.9 6.5 slice-start.19
  1142.3 6.3 slice-start.16
  1143.4 5.1 slice-start.17
  1148.5 5.5 slice-start.14
  1148.5 6.5 slice-start.15
  1154.0 6.2 slice-start.12
  1155.0 5.1 slice-start.13
  1236.8 32.7 %slice-start.8 = ((s8[16777216]{0:T(1024)(128)(4,1)}), s8[4194304]{0:T(1024)(128)(4,1)S(1)}, s32[]{:S(2)}) async-start(s8[16777216]{0:T(1024)(128)(4,1)} %bitcast.64), calls=%async_computation.9 | async-start | bytes 8388608
  1236.8 32.7 %slice-start.9 = ((s8[16777216]{0:T(1024)(128)(4,1)}), s8[4194304]{0:T(1024)(128)(4,1)S(1)}, s32[]{:S(2)}) async-start(s8[16777216]{0:T(1024)(128)(4,1)} %bitcast.64), calls=%async_computation.10 | async-start | bytes 8388608
  1236.8 32.7 %slice-start.10 = ((s8[16777216]{0:T(1024)(128)(4,1)}), s8[4194304]{0:T(1024)(128)(4,1)S(1)}, s32[]{:S(2)}) async-start(s8[16777216]{0:T(1024)(128)(4,1)} %bitcast.64), calls=%async_computation.11 | async-start | bytes 8388608
  1255.5 14.0 %slice-start.11 = ((s8[16777216]{0:T(1024)(128)(4,1)}), s8[4194304]{0:T(1024)(128)(4,1)S(1)}, s32[]{:S(2)}) async-start(s8[16777216]{0:T(1024)(128)(4,1)} %bitcast.64), calls=%async_computation.12 | async-start | bytes 8388608
  1311.7 6.8 copy-start.17
Sparse Core Ops, SparseCore 0:
  168.1 959.1 all-reduce.4
